TPU v7x, 32 devices: a whole 2x2x4 slice. The times are simulated.
32 devices in a mesh: dp: 2 (over x), sp: 4 (over z), tp: 4 (over y, core).
Axes of the slice: x: 2, y: 2, z: 4, core: 2. Of those that a mesh axis runs over, the one named last changes fastest.
Arguments:
- x_in: bfloat16 [256, 3072], P('dp'), parts along dimension 0
- lengths: int32 [256], P('dp'), parts along dimension 0
- w_q: bfloat16 [2, 3072, 3072], P(None, None, 'tp')
- w_k: bfloat16 [2, 3072, 1024], P(None, None, 'tp')
- w_v: bfloat16 [2, 3072, 1024], P(None, None, 'tp')
- w_o: bfloat16 [2, 3072, 3072], P(None, 'tp')
- w_gate: bfloat16 [2, 3072, 8192], P(None, None, 'tp')
- w_up: bfloat16 [2, 3072, 8192], P(None, None, 'tp')
- w_down: bfloat16 [2, 8192, 3072], P(None, 'tp')
- gain_attn: bfloat16 [2, 3072], replicated
- gain_mlp: bfloat16 [2, 3072], replicated
- k_cache: bfloat16 [2, 256, 8, 512, 128], P(None, 'dp', 'tp', 'sp'), parts along dimension 1
- v_cache: bfloat16 [2, 256, 8, 512, 128], P(None, 'dp', 'tp', 'sp'), parts along dimension 1
Outputs:
- output 1: bfloat16 [256, 3072], P('dp'), parts along dimension 0
- output 2: bfloat16 [2, 256, 8, 128], P(None, 'dp', 'tp'), parts along dimension 1
- output 3: bfloat16 [2, 256, 8, 128], P(None, 'dp', 'tp'), parts along dimension 1
There are 2 independent parts. A program takes and returns all parts, laid end to end along the dimension named above; an argument that names none is the same for every part.
All inputs are finite; a program needn't handle non-finite values.
Results may differ from a plain program's by a relative error of at most 0.02.
Values are sent between devices in bfloat16 or wider.
A program may use at most 1 GiB of HBM per device.

v0:
```python
import jax
import jax.numpy as jnp
from jax import lax
from jax.sharding import PartitionSpec as P

EPSILON = 1e-5
NEG_BIG = -1e30


def rms_norm(residual, gain_vec):
    wide_res = residual.astype(jnp.float32)
    mean_sq = jnp.mean(wide_res * wide_res, axis=-1, keepdims=True)
    return (wide_res * lax.rsqrt(mean_sq + EPSILON) * gain_vec.astype(jnp.float32)).astype(jnp.bfloat16)


def local_attention(query_vec, k_layer, v_layer, valid_mask, score_scale):
    scores = jnp.einsum("bkgd,bktd->bkgt", query_vec, k_layer, preferred_element_type=jnp.float32) * score_scale
    scores = jnp.where(valid_mask, scores, NEG_BIG)
    local_max = jnp.max(scores, axis=-1)
    prob_w = jnp.where(valid_mask, jnp.exp(scores - local_max[..., None]), 0.0)
    local_sum = jnp.sum(prob_w, axis=-1)
    local_out = jnp.einsum("bkgt,bktd->bkgd", prob_w.astype(jnp.bfloat16), v_layer, preferred_element_type=jnp.float32)
    return jnp.concatenate([local_out, local_max[..., None], local_sum[..., None]], axis=-1)


def combine_parts(gathered, head_dim, new_score, val_new):
    part_out = gathered[..., :head_dim]
    part_max = gathered[..., head_dim]
    part_sum = gathered[..., head_dim + 1]
    run_max = jnp.maximum(jnp.max(part_max, axis=0), new_score)
    part_wt = jnp.exp(part_max - run_max)
    prob_new = jnp.exp(new_score - run_max)
    denom_sum = jnp.sum(part_wt * part_sum, axis=0) + prob_new
    numer_sum = jnp.sum(part_wt[..., None] * part_out, axis=0)
    numer_sum = numer_sum + prob_new.astype(jnp.bfloat16).astype(jnp.float32)[..., None] * val_new[:, :, None, :].astype(jnp.float32)
    return (numer_sum / denom_sum[..., None]).astype(jnp.bfloat16)


def solution(mesh):
    weight_col = P(None, None, "tp")
    weight_row = P(None, "tp", None)
    cache_spec = P(None, "dp", "tp", "sp", None)
    new_spec = P(None, "dp", "tp", None)

    def device_step(x_in, lengths, w_q, w_k, w_v, w_o, w_gate, w_up, w_down, gain_attn, gain_mlp, k_cache, v_cache):
        n_layers = w_q.shape[0]
        batch_size = x_in.shape[0]
        kv_heads = k_cache.shape[2]
        t_local = k_cache.shape[3]
        head_dim = k_cache.shape[4]
        q_heads = w_q.shape[2] // head_dim
        group_size = q_heads // kv_heads
        score_scale = head_dim ** -0.5
        positions = lax.axis_index("sp") * t_local + jnp.arange(t_local)
        valid_mask = (positions[None, :] < lengths[:, None])[:, None, None, :]
        residual = x_in
        key_list = []
        val_list = []
        for layer_idx in range(n_layers):
            normed = rms_norm(residual, gain_attn[layer_idx])
            query_vec = jnp.dot(normed, w_q[layer_idx], preferred_element_type=jnp.float32).astype(jnp.bfloat16).reshape(batch_size, kv_heads, group_size, head_dim)
            key_new = jnp.dot(normed, w_k[layer_idx], preferred_element_type=jnp.float32).astype(jnp.bfloat16).reshape(batch_size, kv_heads, head_dim)
            val_new = jnp.dot(normed, w_v[layer_idx], preferred_element_type=jnp.float32).astype(jnp.bfloat16).reshape(batch_size, kv_heads, head_dim)
            packed = local_attention(query_vec, k_cache[layer_idx], v_cache[layer_idx], valid_mask, score_scale)
            gathered = lax.all_gather(packed, "sp")
            new_score = jnp.einsum("clhe,cle->clh", query_vec, key_new, preferred_element_type=jnp.float32) * score_scale
            attn_out = combine_parts(gathered, head_dim, new_score, val_new).reshape(batch_size, q_heads * head_dim)
            attn_part = jnp.dot(attn_out, w_o[layer_idx], preferred_element_type=jnp.float32).astype(jnp.bfloat16)
            attn_sum = lax.psum(attn_part, "tp")
            residual = (residual.astype(jnp.float32) + attn_sum.astype(jnp.float32)).astype(jnp.bfloat16)
            normed_mlp = rms_norm(residual, gain_mlp[layer_idx])
            gate_proj = jnp.dot(normed_mlp, w_gate[layer_idx], preferred_element_type=jnp.float32)
            up_proj = jnp.dot(normed_mlp, w_up[layer_idx], preferred_element_type=jnp.float32)
            hidden_act = (jax.nn.silu(gate_proj) * up_proj).astype(jnp.bfloat16)
            mlp_part = jnp.dot(hidden_act, w_down[layer_idx], preferred_element_type=jnp.float32).astype(jnp.bfloat16)
            mlp_sum = lax.psum(mlp_part, "tp")
            residual = (residual.astype(jnp.float32) + mlp_sum.astype(jnp.float32)).astype(jnp.bfloat16)
            key_list.append(key_new)
            val_list.append(val_new)
        return residual, jnp.stack(key_list), jnp.stack(val_list)

    in_specs = (P("dp", None), P("dp"), weight_col, weight_col, weight_col, weight_row, weight_col, weight_col, weight_row, P(None, None), P(None, None), cache_spec, cache_spec)
    out_specs = (P("dp", None), new_spec, new_spec)
    return jax.shard_map(device_step, mesh=mesh, in_specs=in_specs, out_specs=out_specs, check_vma=False)
```

profile of v0, /device:TPU:0, one launch (start us, length us, event | category | flops | bytes accessed | tf_op | source)
XLA Modules:
  0.0 340.6 jit_solution(1815673027816145535)
XLA Ops:
  7.2 0.8 slice_convert_fusion.3
  8.0 1.4 fusion.66
  9.4 3.4 %fusion.102 = bf16[128,768]{1,0:T(8,128)(2,1)S(1)} fusion(bf16[2,3072,768]{2,1,0:T(8,128)(2,1)} %param.15, bf16[128,3072]{1,0:T(8,128)(2,1)} %param.13, f32[3072]{0:T(1024)S(1)} %bitcast.192, f32[128]{0:T(128)S(1)} %add_rsqrt_fusion.3), kind=kOutput, calls=%fused_computation.96 | convolution fusion | flops 605650944 | bytes 5714432 | tf_op jit(solution)/shard_map/dot_general | solution.py:61
  13.3 8.0 %fusion.171 = (f32[128,2,3]{2,1,0:T(2,128)S(1)}, f32[128,2,3,128]{3,2,1,0:T(4,128)S(1)}) fusion(bf16[128,2,3,128]{3,2,1,0:T(4,128)(2,1)S(1)} %copy.77, bf16[2,128,2,128,128]{4,3,2,1,0:T(8,128)(2,1)} %param.24, pred[128,128]{1,0:T(8,128)(4,1)S(1)} %broadcast_compare_fusion), kind=kOutput, calls=%fused_computation.166 | convolution fusion | flops 25459968 | bytes 8997888 | tf_op jit(solution)/shard_map/bkgd,bktd->bkgt/dot_general | solution.py:17
  21.4 0.8 fusion.134
  22.2 5.7 %fusion.22 = f32[128,2,3,128]{3,2,1,0:T(4,128)S(1)} fusion(bf16[2,128,2,128,128]{4,3,2,1,0:T(8,128)(2,1)} %param.25, f32[128,2,3,128]{3,2,1,0:T(4,128)S(1)} %get-tuple-element.22, f32[128,2,3]{2,1,0:T(2,128)S(1)} %get-tuple-element.21, pred[128,128]{1,0:T(8,128)(4,1)S(1)} %broadcast_compare_fusion), kind=kOutput, calls=%fused_computation.22 | convolution fusion | flops 25460736 | bytes 9194496 | tf_op jit(solution)/shard_map/bkgt,bktd->bkgd/dot_general | solution.py:22
  28.3 1.0 pad_maximum_fusion
  29.5 1.8 fusion.108
  31.3 0.4 fusion.173
  31.8 1.9 fusion.111
  33.8 37.7 %all-gather.5.cloned.1.call-done = f32[512,2,3,130]{0,1,3,2:T(2,128)} async-done(((f32[128,2,3,130]{0,1,3,2:T(2,128)}), f32[512,2,3,130]{0,1,3,2:T(2,128)}) %all-gather.5.cloned.1.call-update) | async-done | bytes 1597456 | tf_op jit(solution)/shard_map/all_gather | solution.py:65
  71.5 2.8 reshape.161
  74.6 0.8 copy.84
  75.4 1.8 fusion.83
  77.2 1.2 copy.102
  78.5 1.6 fusion.132
  80.3 4.0 %fusion.48 = bf16[128,3072]{1,0:T(8,128)(2,1)} fusion(bf16[128,768]{0,1:T(8,128)(2,1)S(1)} %bitcast.181, bf16[2,768,3072]{2,1,0:T(8,128)(2,1)} %param.18), kind=kOutput, calls=%fused_computation.44 | convolution fusion | flops 604372992 | bytes 5701632 | tf_op jit(solution)/shard_map/dot_general | solution.py:68
  84.4 33.2 %all-reduce.5.cloned.1.call-done = bf16[128,3072]{1,0:T(8,128)(2,1)} async-done(((bf16[128,3072]{1,0:T(8,128)(2,1)}), bf16[128,3072]{1,0:T(8,128)(2,1)}) %all-reduce.5.cloned.1.call-update) | async-done | bytes 786448 | tf_op jit(solution)/shard_map/psum | solution.py:69
  117.6 1.5 fusion.70
  119.1 5.7 %fusion.10 = f32[128,2048]{1,0:T(8,128)S(1)} fusion(bf16[2,3072,2048]{2,1,0:T(8,128)(2,1)} %param.19, bf16[128,3072]{1,0:T(8,128)(2,1)S(1)} %get-tuple-element.6, f32[3072]{0:T(1024)S(1)} %bitcast.195, f32[128]{0:T(128)S(1)} %add_rsqrt_fusion.2), kind=kOutput, calls=%fused_computation.10 | convolution fusion | flops 1612185600 | bytes 14430720 | tf_op jit(solution)/shard_map/dot_general | solution.py:72
  124.8 11.2 %fusion.42 = bf16[128,3072]{1,0:T(8,128)(2,1)} fusion(bf16[2,2048,3072]{2,1,0:T(8,128)(2,1)} %param.21, bf16[2,3072,2048]{2,1,0:T(8,128)(2,1)} %param.20, f32[128,2048]{1,0:T(8,128)S(1)} %fusion.10, bf16[128,3072]{1,0:T(8,128)(2,1)S(1)} %get-tuple-element.6, f32[3072]{0:T(1024)S(1)} %bitcast.196, f32[128]{0:T(128)S(1)} %add_rsqrt_fusion.2), kind=kOutput, calls=%fused_computation.42 | convolution fusion | flops 3224764416 | bytes 27800064 | tf_op jit(solution)/shard_map/dot_general | solution.py:75
  136.3 34.8 %all-reduce.7.cloned.1.call-done = bf16[128,3072]{1,0:T(8,128)(2,1)} async-done(((bf16[128,3072]{1,0:T(8,128)(2,1)}), bf16[128,3072]{1,0:T(8,128)(2,1)}) %all-reduce.7.cloned.1.call-update) | async-done | bytes 786448 | tf_op jit(solution)/shard_map/psum | solution.py:76
  171.0 1.5 fusion.74
  172.6 0.3 fusion.76
  172.9 3.1 fusion.105
  176.4 8.0 %fusion.172 = (f32[128,2,3]{2,1,0:T(2,128)S(1)}, f32[128,2,3,128]{3,2,1,0:T(4,128)S(1)}) fusion(bf16[128,2,3,128]{3,2,1,0:T(4,128)(2,1)S(1)} %copy.87, bf16[2,128,2,128,128]{4,3,2,1,0:T(8,128)(2,1)} %param.24, pred[128,128]{1,0:T(8,128)(4,1)S(1)} %broadcast_compare_fusion), kind=kOutput, calls=%fused_computation.167 | convolution fusion | flops 25459968 | bytes 8997888 | tf_op jit(solution)/shard_map/bkgd,bktd->bkgt/dot_general | solution.py:17
  184.5 5.7 %fusion.18 = f32[128,2,3,128]{3,2,1,0:T(4,128)S(1)} fusion(bf16[2,128,2,128,128]{4,3,2,1,0:T(8,128)(2,1)} %param.25, f32[128,2,3,128]{3,2,1,0:T(4,128)S(1)} %get-tuple-element.24, f32[128,2,3]{2,1,0:T(2,128)S(1)} %get-tuple-element.23, pred[128,128]{1,0:T(8,128)(4,1)S(1)} %broadcast_compare_fusion), kind=kOutput, calls=%fused_computation.18 | convolution fusion | flops 25460736 | bytes 9194496 | tf_op jit(solution)/shard_map/bkgt,bktd->bkgd/dot_general | solution.py:22
  190.2 0.8 fusion.136
  191.4 1.0 pad_maximum_fusion.1
  192.4 0.3 all-reduce.9.cloned.1.call-start
  192.7 1.8 fusion.114
  194.6 0.4 fusion.174
  195.1 1.8 fusion.117
  197.0 0.5 copy-done.8
  197.5 34.4 %all-gather.7.cloned.1.call-done = f32[512,2,3,130]{0,1,3,2:T(2,128)} async-done(((f32[128,2,3,130]{0,1,3,2:T(2,128)}), f32[512,2,3,130]{0,1,3,2:T(2,128)}) %all-gather.7.cloned.1.call-update) | async-done | bytes 1597456 | tf_op jit(solution)/shard_map/all_gather | solution.py:65
  231.9 2.8 reshape.164
  235.0 0.8 copy.94
  235.8 1.8 fusion.82
  237.6 1.2 copy.103
  238.9 1.6 fusion.133
  240.7 4.0 %fusion.51 = bf16[128,3072]{1,0:T(8,128)(2,1)} fusion(bf16[128,768]{0,1:T(8,128)(2,1)S(1)} %bitcast.182, bf16[2,768,3072]{2,1,0:T(8,128)(2,1)} %param.18), kind=kOutput, calls=%fused_computation.45 | convolution fusion | flops 604372992 | bytes 5701632 | tf_op jit(solution)/shard_map/dot_general | solution.py:68
  244.8 33.3 %all-reduce.9.cloned.1.call-done = bf16[128,3072]{1,0:T(8,128)(2,1)} async-done(((bf16[128,3072]{1,0:T(8,128)(2,1)}), bf16[128,3072]{1,0:T(8,128)(2,1)}) %all-reduce.9.cloned.1.call-update) | async-done | bytes 786448 | tf_op jit(solution)/shard_map/psum | solution.py:69
  278.0 1.6 fusion.78
  279.6 5.7 %fusion.4 = f32[128,2048]{1,0:T(8,128)S(1)} fusion(bf16[2,3072,2048]{2,1,0:T(8,128)(2,1)} %param.19, bf16[128,3072]{1,0:T(8,128)(2,1)S(1)} %get-tuple-element.4, f32[3072]{0:T(1024)S(1)} %bitcast.190, f32[128]{0:T(128)S(1)} %add_rsqrt_fusion), kind=kOutput, calls=%fused_computation.4 | convolution fusion | flops 1612185600 | bytes 14430720 | tf_op jit(solution)/shard_map/dot_general | solution.py:72
  285.4 11.2 %fusion.45 = bf16[128,3072]{1,0:T(8,128)(2,1)} fusion(bf16[2,2048,3072]{2,1,0:T(8,128)(2,1)} %param.21, bf16[2,3072,2048]{2,1,0:T(8,128)(2,1)} %param.20, f32[128,2048]{1,0:T(8,128)S(1)} %fusion.4, bf16[128,3072]{1,0:T(8,128)(2,1)S(1)} %get-tuple-element.4, f32[3072]{0:T(1024)S(1)} %bitcast.191, f32[128]{0:T(128)S(1)} %add_rsqrt_fusion), kind=kOutput, calls=%fused_computation.43 | convolution fusion | flops 3224764416 | bytes 27800064 | tf_op jit(solution)/shard_map/dot_general | solution.py:75
  296.7 1.1 pad_maximum_fusion.2
  297.7 33.8 %all-reduce.11.cloned.1.call-done = bf16[128,3072]{1,0:T(8,128)(2,1)} async-done(((bf16[128,3072]{1,0:T(8,128)(2,1)}), bf16[128,3072]{1,0:T(8,128)(2,1)}) %all-reduce.11.cloned.1.call-update) | async-done | bytes 786448 | tf_op jit(solution)/shard_map/psum | solution.py:76
  331.6 2.2 fusion.81
  (75 shorter events, 3.8 us)
Async XLA Ops:
  7.2 64.3 %all-gather.5.cloned.1.call-start = ((), (), s32[]{:S(2)}) async-start(), calls=%async_computation.4 | async-start | bytes 1996800 | tf_op jit(solution)/shard_map/all_gather | solution.py:65
  9.4 3.8 %copy-start.11 = (s32[128]{0:T(128)S(1)}, s32[128]{0:T(128)}, u32[]{:S(2)}) copy-start(s32[128]{0:T(128)} %param.14) | copy-start | bytes 1540
  27.9 1.5 copy-start.1
  29.2 88.4 %all-reduce.5.cloned.1.call-start = ((), (), s32[]{:S(2)}) async-start(), calls=%async_computation | async-start | bytes 1572864 | tf_op jit(solution)/shard_map/psum | solution.py:69
  33.7 40.6 %copy-start.4 = (bf16[128,256]{1,0:T(8,128)(2,1)}, bf16[128,256]{1,0:T(8,128)(2,1)S(1)}, u32[]{:S(2)}) copy-start(bf16[128,256]{1,0:T(8,128)(2,1)S(1)} %fusion.111) | copy-start | bytes 196612
  80.2 4.1 %copy-start.10 = (bf16[2,3072]{1,0:T(2,128)(2,1)S(1)}, bf16[2,3072]{1,0:T(2,128)(2,1)}, u32[]{:S(2)}) copy-start(bf16[2,3072]{1,0:T(2,128)(2,1)} %param.23) | copy-start | bytes 36868
  84.3 86.7 %all-reduce.7.cloned.1.call-start = ((), (), s32[]{:S(2)}) async-start(), calls=%async_computation.1 | async-start | bytes 1572864 | tf_op jit(solution)/shard_map/psum | solution.py:76
  136.0 95.9 %all-gather.7.cloned.1.call-start = ((), (), s32[]{:S(2)}) async-start(), calls=%async_computation.5 | async-start | bytes 1996800 | tf_op jit(solution)/shard_map/all_gather | solution.py:65
  171.0 1.6 copy-start
  176.4 8.1 %copy-start.2 = (bf16[128,2,3,128]{3,2,1,0:T(4,128)(2,1)}, bf16[128,2,3,128]{3,2,1,0:T(4,128)(2,1)S(1)}, u32[]{:S(2)}) copy-start(bf16[128,2,3,128]{3,2,1,0:T(4,128)(2,1)S(1)} %copy.87) | copy-start | bytes 589828
  192.4 2.2 copy-start.3
  192.4 85.6 %all-reduce.9.cloned.1.call-start = ((), (), s32[]{:S(2)}) async-start(), calls=%async_computation.2 | async-start | bytes 1572864 | tf_op jit(solution)/shard_map/psum | solution.py:69
  194.5 2.4 copy-start.6
  196.9 0.6 copy-start.8
  244.7 86.8 %all-reduce.11.cloned.1.call-start = ((), (), s32[]{:S(2)}) async-start(), calls=%async_computation.3 | async-start | bytes 1572864 | tf_op jit(solution)/shard_map/psum | solution.py:76
  285.3 11.2 %copy-start.5 = (bf16[128,256]{1,0:T(8,128)(2,1)S(1)}, bf16[128,256]{1,0:T(8,128)(2,1)}, u32[]{:S(2)}) copy-start(bf16[128,256]{1,0:T(8,128)(2,1)} %copy-done.4) | copy-start | bytes 196612
  285.3 11.3 %copy-start.7 = (bf16[128,256]{1,0:T(8,128)(2,1)S(1)}, bf16[128,256]{1,0:T(8,128)(2,1)}, u32[]{:S(2)}) copy-start(bf16[128,256]{1,0:T(8,128)(2,1)} %copy-done.6) | copy-start | bytes 196612
  285.3 11.3 %copy-start.9 = (bf16[128,256]{1,0:T(8,128)(2,1)S(1)}, bf16[128,256]{1,0:T(8,128)(2,1)}, u32[]{:S(2)}) copy-start(bf16[128,256]{1,0:T(8,128)(2,1)} %copy-done.8) | copy-start | bytes 196612
Sparse Core Ops, SparseCore 0:
  29.4 42.0 all-gather.4
  84.4 33.1 all-reduce.4
  136.1 34.8 all-reduce.6
  192.5 39.3 all-gather.6
  244.9 33.1 all-reduce.8
  296.7 34.8 all-reduce.10
where the time goes:
time: 342 us; the launch traced here: 341 us
  waiting for transfers between devices  207 us (61%)
  matrix products  83.8 us (25%)
  other arithmetic  21 us (6%)
  between operations  14.6 us (4%)
  local copies, waits for them, and re-layouts  13.1 us (4%)
    all_gather x2, waiting for transfers between devices, device_step(): gathered = lax.all_gather(packed, 'sp')  72.1 us
    psum x2, waiting for transfers between devices, device_step(): mlp_sum = lax.psum(mlp_part, 'tp')  68.6 us
    psum x2, waiting for transfers between devices, device_step(): attn_sum = lax.psum(attn_part, 'tp')  66.5 us
    dot_general x2, matrix products, device_step(): jnp.dot(hidden_act, w_down[layer_idx], preferred_element_type=jnp.float32)  22.3 us
    dot_general x2, matrix products, local_attention(): jnp.einsum('bkgd,bktd->bkgt', query_vec, k_layer, preferred_element_type=...  16 us
    dot_general x2, matrix products, local_attention(): jnp.einsum('bkgt,bktd->bkgd', prob_w.astype(jnp.bfloat16), v_layer, prefe...  11.4 us
    dot_general x2, matrix products, device_step(): jnp.dot(normed_mlp, w_gate[layer_idx], preferred_element_type=jnp.float32)  11.3 us
    dot_general x2, matrix products, device_step(): jnp.dot(attn_out, w_o[layer_idx], preferred_element_type=jnp.float32)  8.07 us
  transfers between devices with their start and end apart: 6, of which 6 were waited for; matrix products, arithmetic and copies ran while one was open for 3% of the time, Pallas kernels for 0%

commit v1 on v0

v1 whole, which is shorter than its diff:
```python
import functools

import jax
import jax.numpy as jnp
from jax import lax
from jax.experimental import pallas as pl
from jax.experimental.pallas import tpu as pltpu
from jax.sharding import PartitionSpec as P

MESH = pl.DeviceIdType.MESH
EPSILON = 1e-5
NEG_BIG = -1e30
BF = jnp.bfloat16
F32 = jnp.float32


def dot(a, b):
    return jnp.dot(a, b, preferred_element_type=F32)


def dot_t(a, b):
    return lax.dot_general(a, b, (((1,), (1,)), ((), ())), preferred_element_type=F32)


def kernel(cfg, lens, x_hbm, wq, wk, wv, wo, wg, wu, wd, ga, gm, kc, vc, x_out, k_out, v_out, *scratch):
    (gu, kb, vb, wob, wdb, xbuf, hbuf, acc, qown, qrecv, qs, os, oown, osend, orecv, stsend, strecv, attn, act,
     msend, mrecv, ysend, yrecv, s_qkv, s_kv, s_w, s_gu, q_s, q_r, kv_s, kv_r, o_s, o_r, st_s, st_r,
     m_s, m_r, y_s, y_r, x_s, x_r, f_s, f_r, g_s, g_r) = scratch
    n_layers, n_sp, rows, d_model, q_cols, kv_cols, ff, dh = cfg
    n_q = q_cols // dh
    n_kv = kv_cols // dh
    group = n_q // n_kv
    t_loc = kb.shape[1] // rows // n_kv
    z = lax.axis_index("sp")
    t = lax.axis_index("tp")
    core = lax.rem(t, 2)
    mate = t + 1 - 2 * core
    ypeer = lax.rem(t + 2, 4)
    half = d_model // 2
    n_ch = 2
    ch_w = half // n_ch
    k_ch = 4
    k_w = d_model // k_ch
    scale = dh ** -0.5
    order = (0, 1, 3, 2)

    def up(d):
        return lax.rem(z + d, n_sp)

    def down(d):
        return lax.rem(z + n_sp - d, n_sp)

    def row_ds(src):
        return pl.ds(pl.multiple_of(src * rows, rows), rows)

    def rcopy(src, dst, ss, rs, **dev):
        return pltpu.make_async_remote_copy(src_ref=src, dst_ref=dst, send_sem=ss, recv_sem=rs, device_id=dev, device_id_type=MESH)

    def qkv_copies(l):
        out = []
        for c in range(k_ch):
            r = pl.ds(c * k_w, k_w)
            out.append((
                pltpu.make_async_copy(wq.at[l, r, :], gu.at[r, pl.ds(0, q_cols)], s_qkv.at[c, 0]),
                pltpu.make_async_copy(wk.at[l, r, :], gu.at[r, pl.ds(q_cols, kv_cols)], s_qkv.at[c, 1]),
                pltpu.make_async_copy(wv.at[l, r, :], gu.at[r, pl.ds(q_cols + kv_cols, kv_cols)], s_qkv.at[c, 2]),
            ))
        return out

    def kv_copies(l, j):
        src = pl.multiple_of(down(order[j]) * kb.shape[1], kb.shape[1])
        r = pl.ds(src, kb.shape[1])
        return (pltpu.make_async_copy(kc.at[l, r, :], kb.at[j], s_kv.at[j, 0]),
                pltpu.make_async_copy(vc.at[l, r, :], vb.at[j], s_kv.at[j, 1]))

    def gu_copies(l):
        return (pltpu.make_async_copy(wg.at[l], gu.at[:, pl.ds(0, ff)], s_gu.at[0]),
                pltpu.make_async_copy(wu.at[l], gu.at[:, pl.ds(ff, ff)], s_gu.at[1]))

    def wo_copy(l):
        return pltpu.make_async_copy(wo.at[l], wob, s_w.at[0])

    def wd_copy(l):
        return pltpu.make_async_copy(wd.at[l], wdb, s_w.at[1])

    x_copy = pltpu.make_async_copy(x_hbm.at[row_ds(z), :], xbuf.at[0], s_w.at[2])

    def start_qkv(l):
        for c in qkv_copies(l):
            for cp in c:
                cp.start()

    def start_kv(l):
        for j in range(n_sp):
            for cp in kv_copies(l, j):
                cp.start()

    x_copy.start()
    start_qkv(0)
    start_kv(0)
    wo_copy(0).start()

    barrier = pltpu.get_barrier_semaphore()
    for d in range(1, n_sp):
        pl.semaphore_signal(barrier, inc=1, device_id={"sp": up(d)}, device_id_type=MESH)
    pl.semaphore_signal(barrier, inc=1, device_id={"tp": mate}, device_id_type=MESH)
    pl.semaphore_signal(barrier, inc=1, device_id={"tp": ypeer}, device_id_type=MESH)

    qs[...] = jnp.zeros_like(qs)
    row_i = lax.broadcasted_iota(jnp.int32, (8, dh), 0)
    lane_i = lax.broadcasted_iota(jnp.int32, (8, dh), 1)
    lane_r = lax.broadcasted_iota(jnp.int32, (rows, dh), 1)
    first_kv = row_i < group

    pending = []
    reuse = ([], [])

    def send(cp):
        cp.start()
        pending.append(cp)

    def norm(src_ref, gain_row):
        w = 512
        tot = jnp.zeros((rows, 128), F32)
        for c in range(d_model // 128):
            xw = src_ref[:, c * 128:(c + 1) * 128].astype(F32)
            tot = tot + xw * xw
        inv = lax.rsqrt(jnp.sum(tot, axis=-1, keepdims=True) / d_model + EPSILON)
        for c in range(d_model // w):
            cols = slice(c * w, (c + 1) * w)
            hbuf[:, cols] = (src_ref[:, cols].astype(F32) * inv * gain_row[:, cols].astype(F32)).astype(BF)

    def attend(l, j):
        src = down(order[j])
        base = src * rows
        for cp in kv_copies(l, j):
            cp.wait()
        unroll = 8

        def body(i, carry):
            st_m, st_s = carry
            ps = []
            for u in range(unroll):
                b = i * unroll + u
                q = qs[pl.ds(pl.multiple_of(b * 8, 8), 8), :].astype(BF)
                k = kb[j, pl.ds(pl.multiple_of(b * n_kv * t_loc, n_kv * t_loc), n_kv * t_loc), :]
                s2 = dot_t(q, k)
                s = jnp.where(first_kv, s2[:, :t_loc], s2[:, t_loc:]) * scale
                mask = (z * t_loc + lane_i) < lens[base + b]
                s = jnp.where(mask, s, NEG_BIG)
                m = jnp.max(s, axis=1, keepdims=True)
                p = jnp.where(mask, jnp.exp(s - m), 0.0)
                tot = jnp.sum(p, axis=1, keepdims=True)
                st_m = jnp.where(lane_i == b, m, st_m)
                st_s = jnp.where(lane_i == b, tot, st_s)
                ps.append(jnp.concatenate([jnp.where(first_kv, p, 0.0), jnp.where(first_kv, 0.0, p)], axis=1).astype(BF))
            for u in range(unroll):
                b = i * unroll + u
                v = vb[j, pl.ds(pl.multiple_of(b * n_kv * t_loc, n_kv * t_loc), n_kv * t_loc), :]
                os[pl.ds(pl.multiple_of(b * 8, 8), 8), :] = dot(ps[u], v)
            return st_m, st_s

        zero = jnp.zeros((8, dh), F32)
        st_m, st_s = lax.fori_loop(0, rows // unroll, body, (zero, zero))
        return jnp.concatenate([st_m, st_s, jnp.zeros((dh - 16, dh), F32)], axis=0).T[:rows, :]

    def reduce(stage, lhs, w_ref, last):
        def part(col):
            return dot(lhs[...], w_ref[:, pl.ds(pl.multiple_of(col, 128), ch_w)])

        m_cp, y_cp = [], []
        par = stage % 2
        for cp in reuse[par]:
            cp.wait_send()
        reuse[par].clear()
        for c in range(n_ch):
            msend[par, c] = part((1 - core) * half + c * ch_w).astype(BF)
            cp = rcopy(msend.at[par, c], mrecv.at[par, c], m_s.at[stage, c], m_r.at[stage, c], tp=mate)
            cp.start()
            reuse[par].append(cp)
            m_cp.append(cp)
        for c in range(n_ch):
            p = part(core * half + c * ch_w)
            m_cp[c].wait_recv()
            ysend[par, c] = (p + mrecv[par, c].astype(F32)).astype(BF)
            cp = rcopy(ysend.at[par, c], yrecv.at[par, c], y_s.at[stage, c], y_r.at[stage, c], tp=ypeer)
            cp.start()
            reuse[par].append(cp)
            y_cp.append(cp)
        x_cp = []
        for c in range(n_ch):
            cols = pl.ds(pl.multiple_of(core * half + c * ch_w, 128), ch_w)
            y_cp[c].wait_recv()
            tot = ysend[par, c].astype(F32) + yrecv[par, c].astype(F32)
            new = (xbuf[stage, :, cols].astype(F32) + tot).astype(BF)
            if last:
                dst = x_out.at[row_ds(z), cols]
            else:
                dst = xbuf.at[stage + 1, :, cols]
            dst[...] = new
            cp = rcopy(dst, dst, x_s.at[stage, c], x_r.at[stage, c], tp=mate)
            send(cp)
            x_cp.append(cp)
            if last:
                for d in (2, 1, 3):
                    send(rcopy(dst, dst, f_s.at[d - 1, c], f_r.at[d - 1, c], sp=up(d)))
        if last:
            for d in (1, 3, 2):
                for c in range(n_ch):
                    cols = pl.ds(pl.multiple_of(core * half + c * ch_w, 128), ch_w)
                    dst = x_out.at[row_ds(down(d)), cols]
                    rcopy(dst, dst, f_s.at[d - 1, c], f_r.at[d - 1, c], sp=up(d)).wait_recv()
                    send(rcopy(dst, dst, g_s.at[d - 1, c], g_r.at[d - 1, c], tp=mate))
        for cp in x_cp:
            cp.wait_recv()
        if last:
            for d in (1, 3, 2):
                for c in range(n_ch):
                    cols = pl.ds(pl.multiple_of((1 - core) * half + c * ch_w, 128), ch_w)
                    dst = x_out.at[row_ds(down(d)), cols]
                    rcopy(dst, dst, g_s.at[d - 1, c], g_r.at[d - 1, c], tp=mate).wait_recv()

    for l in range(n_layers):
        if l == 0:
            x_copy.wait()
        norm(xbuf.at[2 * l], ga[l:l + 1, :])
        for c, cps in enumerate(qkv_copies(l)):
            for cp in cps:
                cp.wait()
            r = pl.ds(c * k_w, k_w)
            val = dot(hbuf[:, r], gu[r, pl.ds(0, q_cols + 2 * kv_cols)])
            if c == 0:
                acc[...] = val
            else:
                acc[...] += val
        for cp in gu_copies(l):
            cp.start()
        if l == 0:
            wd_copy(0).start()
        if l == 0:
            pl.semaphore_wait(barrier, n_sp - 1 + 2)
        for h in range(n_q):
            qown[l, h] = acc[:, h * dh:(h + 1) * dh].astype(BF)
        q_cp = {}
        for d in (2, 1, 3):
            q_cp[d] = rcopy(qown.at[l], qrecv.at[l, d - 1], q_s.at[l, d - 1], q_r.at[l, d - 1], sp=up(d))
            send(q_cp[d])
        own = row_ds(z)
        k_out[l, own, :] = acc[:, q_cols:q_cols + kv_cols].astype(BF)
        v_out[l, own, :] = acc[:, q_cols + kv_cols:].astype(BF)
        kv_cp = []
        for d in (2, 1, 3):
            for i, ref in enumerate((k_out, v_out)):
                cp = rcopy(ref.at[l, own, :], ref.at[l, own, :], kv_s.at[l, d - 1, i], kv_r.at[l, d - 1, i], sp=up(d))
                send(cp)
                kv_cp.append((d, i, ref))

        o_cp = {}
        stats_own = None
        for j in range(n_sp):
            d = order[j]
            q_src = qown.at[l] if d == 0 else qrecv.at[l, d - 1]
            if d:
                q_cp[d].wait_recv()
            for h in range(n_q):
                qs[pl.ds(h, rows, stride=8), :] = q_src[h].astype(F32)
            st = attend(l, j)
            if d == 0:
                stats_own = st
                for h in range(n_q):
                    oown[h] = os[pl.ds(h, rows, stride=8), :]
            else:
                for h in range(n_q):
                    osend[l, d - 1, h] = os[pl.ds(h, rows, stride=8), :].astype(BF)
                stsend[l, d - 1] = st
                a = rcopy(osend.at[l, d - 1], orecv.at[l, d - 1], o_s.at[l, d - 1], o_r.at[l, d - 1], sp=down(d))
                b = rcopy(stsend.at[l, d - 1], strecv.at[l, d - 1], st_s.at[l, d - 1], st_r.at[l, d - 1], sp=down(d))
                send(b)
                send(a)
                o_cp[d] = (a, b)
        if l + 1 < n_layers:
            start_kv(l + 1)

        new_s = jnp.zeros((rows, dh), F32)
        for h in range(n_q):
            g = h // group
            qh = qown[l, h].astype(F32)
            kh = k_out[l, own, g * dh:(g + 1) * dh].astype(F32)
            new_s = jnp.where(lane_r == h, jnp.sum(qh * kh, axis=1, keepdims=True) * scale, new_s)
        for d in range(1, n_sp):
            o_cp[d][1].wait_recv()
        stats = [stats_own] + [strecv[l, d - 1] for d in range(1, n_sp)]
        top = new_s
        for st in stats:
            top = jnp.maximum(top, st)
        p_new = jnp.exp(new_s - top)
        wts = [jnp.exp(st - top) for st in stats]
        denom = p_new
        for st, w in zip(stats, wts):
            denom = denom + w * pltpu.roll(st, dh - 8, 1)
        wts = [w / denom for w in wts]
        w_new = p_new.astype(BF).astype(F32) / denom
        for d in range(1, n_sp):
            o_cp[d][0].wait_recv()
        for h in range(n_q):
            g = h // group
            o = wts[0][:, h:h + 1] * oown[h]
            for d in range(1, n_sp):
                o = o + wts[d][:, h:h + 1] * orecv[l, d - 1, h].astype(F32)
            o = o + w_new[:, h:h + 1] * v_out[l, own, g * dh:(g + 1) * dh].astype(F32)
            attn[:, h * dh:(h + 1) * dh] = o.astype(BF)

        wo_copy(l).wait()
        reduce(2 * l, attn, wob, False)
        if l + 1 < n_layers:
            wo_copy(l + 1).start()
        norm(xbuf.at[2 * l + 1], gm[l:l + 1, :])
        for cp in gu_copies(l):
            cp.wait()
        f_w = 256

        def mlp_body(i, carry):
            c0 = pl.multiple_of(i * f_w, f_w)
            gate = dot(hbuf[...], gu[:, pl.ds(c0, f_w)])
            upv = dot(hbuf[...], gu[:, pl.ds(pl.multiple_of(ff + i * f_w, f_w), f_w)])
            act[:, pl.ds(c0, f_w)] = (gate * jax.nn.sigmoid(gate) * upv).astype(BF)
            return carry

        lax.fori_loop(0, ff // f_w, mlp_body, 0)
        if l + 1 < n_layers:
            start_qkv(l + 1)
        wd_copy(l).wait()
        reduce(2 * l + 1, act, wdb, l == n_layers - 1)
        if l + 1 < n_layers:
            wd_copy(l + 1).start()
        for d, i, ref in kv_cp:
            dst = ref.at[l, row_ds(down(d)), :]
            rcopy(dst, dst, kv_s.at[l, d - 1, i], kv_r.at[l, d - 1, i], sp=up(d)).wait_recv()

    for cp in pending + reuse[0] + reuse[1]:
        cp.wait_send()


def solution(mesh):
    n_sp = mesh.shape["sp"]
    weight_col = P(None, None, "tp")
    weight_row = P(None, "tp", None)
    cache_spec = P(None, "dp", "tp", "sp", None)
    new_spec = P(None, "dp", "tp", None)

    def device_step(x_in, lengths, w_q, w_k, w_v, w_o, w_gate, w_up, w_down, gain_attn, gain_mlp, k_cache, v_cache):
        n_l, batch, n_kv, t_loc, dh = k_cache.shape
        d_model = x_in.shape[1]
        rows = batch // n_sp
        q_cols, kv_cols, ff = w_q.shape[2], w_k.shape[2], w_gate.shape[2]
        n_q = q_cols // dh
        kc = k_cache.reshape(n_l, batch * n_kv * t_loc, dh)
        vc = v_cache.reshape(n_l, batch * n_kv * t_loc, dh)
        cfg = (n_l, n_sp, rows, d_model, q_cols, kv_cols, ff, dh)
        stages = 2 * n_l
        half = d_model // 2
        dma = pltpu.SemaphoreType.DMA
        any_spec = pl.BlockSpec(memory_space=pl.ANY)
        vmem = pl.BlockSpec(memory_space=pltpu.VMEM)
        o3 = n_sp - 1
        scratch = [
            pltpu.VMEM((d_model, 2 * ff), BF),
            pltpu.VMEM((n_sp, rows * n_kv * t_loc, dh), BF),
            pltpu.VMEM((n_sp, rows * n_kv * t_loc, dh), BF),
            pltpu.VMEM((q_cols, d_model), BF),
            pltpu.VMEM((ff, d_model), BF),
            pltpu.VMEM((stages, rows, d_model), BF),
            pltpu.VMEM((rows, d_model), BF),
            pltpu.VMEM((rows, q_cols + 2 * kv_cols), F32),
            pltpu.VMEM((n_l, n_q, rows, dh), BF),
            pltpu.VMEM((n_l, o3, n_q, rows, dh), BF),
            pltpu.VMEM((rows * 8, dh), F32),
            pltpu.VMEM((rows * 8, dh), F32),
            pltpu.VMEM((n_q, rows, dh), F32),
            pltpu.VMEM((n_l, o3, n_q, rows, dh), BF),
            pltpu.VMEM((n_l, o3, n_q, rows, dh), BF),
            pltpu.VMEM((n_l, o3, rows, dh), F32),
            pltpu.VMEM((n_l, o3, rows, dh), F32),
            pltpu.VMEM((rows, q_cols), BF),
            pltpu.VMEM((rows, ff), BF),
        ] + [pltpu.VMEM((2, 2, rows, half // 2), BF)] * 4 + [
            dma((4, 3)), dma((n_sp, 2)), dma((3,)), dma((2,)),
            dma((n_l, o3)), dma((n_l, o3)), dma((n_l, o3, 2)), dma((n_l, o3, 2)),
            dma((n_l, o3)), dma((n_l, o3)), dma((n_l, o3)), dma((n_l, o3)),
            dma((stages, 2)), dma((stages, 2)), dma((stages, 2)), dma((stages, 2)), dma((stages, 2)), dma((stages, 2)),
            dma((o3, 2)), dma((o3, 2)), dma((o3, 2)), dma((o3, 2)),
        ]
        x_out, k_new, v_new = pl.pallas_call(
            functools.partial(kernel, cfg),
            out_shape=(
                jax.ShapeDtypeStruct((batch, d_model), BF),
                jax.ShapeDtypeStruct((n_l, batch, kv_cols), BF),
                jax.ShapeDtypeStruct((n_l, batch, kv_cols), BF),
            ),
            in_specs=[pl.BlockSpec(memory_space=pltpu.SMEM)] + [any_spec] * 8 + [vmem, vmem] + [any_spec] * 2,
            out_specs=(vmem, vmem, vmem),
            scratch_shapes=scratch,
            compiler_params=pltpu.CompilerParams(collective_id=0, has_side_effects=True, vmem_limit_bytes=67043328),
        )(lengths, x_in, w_q, w_k, w_v, w_o, w_gate, w_up, w_down, gain_attn, gain_mlp, kc, vc)
        return x_out, k_new.reshape(n_l, batch, n_kv, dh), v_new.reshape(n_l, batch, n_kv, dh)

    in_specs = (P("dp", None), P("dp"), weight_col, weight_col, weight_col, weight_row, weight_col, weight_col, weight_row, P(None, None), P(None, None), cache_spec, cache_spec)
    out_specs = (P("dp", None), new_spec, new_spec)
    return jax.shard_map(device_step, mesh=mesh, in_specs=in_specs, out_specs=out_specs, check_vma=False)
```

time: 342 us -> 103 us (0.30)
  waiting for transfers between devices: 207 us -> 0 us
  Pallas kernels: 0 us -> 96.4 us
  matrix products: 83.8 us -> 0 us
  other arithmetic: 21 us -> 0 us
  between operations: 14.6 us -> 0.65 us
  local copies, waits for them, and re-layouts: 13.1 us -> 5.25 us
    psum x4 -> x0, waiting for transfers between devices: 135 us -> none  [the longest x2 68.6 us: device_step(): mlp_sum = lax.psum(mlp_part, 'tp')]
    pallas_call x0 -> x1, Pallas kernels: none -> 96.4 us  [device_step(): pl.pallas_call(functools.partial(kernel, cfg), out_shape=(jax.ShapeDtypeS...]
    dot_general x18 -> x0, matrix products: 83.8 us -> none  [the longest x2 22.3 us: device_step(): jnp.dot(hidden_act, w_down[layer_idx], preferred_element_type=jnp.float32)]
    all_gather x2 -> x0, waiting for transfers between devices: 72.1 us -> none  [device_step(): gathered = lax.all_gather(packed, 'sp')]
    reduce_sum x10 -> x0, other arithmetic: 11.3 us -> none  [the longest x4 6 us: rms_norm(): mean_sq = jnp.mean(wide_res * wide_res, axis=-1, keepdims=True)]
    convert_element_type x6 -> x0, other arithmetic: 5.67 us -> none  [the longest x2 3.14 us: combine_parts(): return (numer_sum / denom_sum[..., None]).astype(jnp.bfloat16)]
    all_gather x2 -> x0, local copies, waits for them, and re-layouts: 5.67 us -> none  [device_step(): gathered = lax.all_gather(packed, 'sp')]
  transfers between devices with their start and end apart: 6 -> 0, of which waited for: 6 -> 0; matrix products, arithmetic and copies ran while one was open for 3% -> 0% of each run, Pallas kernels for 0% -> 0%
where the time goes in v1:
time: 103 us; the launch traced here: 102 us
  Pallas kernels  96.4 us (94%)
  local copies, waits for them, and re-layouts  5.25 us (5%)
    pallas_call x1, Pallas kernels, device_step(): pl.pallas_call(functools.partial(kernel, cfg), out_shape=(jax.ShapeDtypeS...  96.4 us
    unnamed x1, local copies, waits for them, and re-layouts  2.06 us

profile of v1, /device:TPU:0, one launch (start us, length us, event | category | flops | bytes accessed | tf_op | source)
XLA Modules:
  0.0 102.3 jit_solution(8618925904051321738)
XLA Ops:
  0.6 96.4 %shard_map.148 = (bf16[128,3072]{1,0:T(8,128)(2,1)}, bf16[2,128,256]{2,1,0:T(8,128)(2,1)}, bf16[2,128,256]{2,1,0:T(8,128)(2,1)}) custom-call(s32[128]{0:T(128)} %lens.1, bf16[128,3072]{1,0:T(8,128)(2,1)} %x_hbm.1, bf16[2,3072,768]{2,1,0:T(8,128)(2,1)} %wq.1, bf16[2,3072,256]{2,1,0:T(8,128)(2,1)} %wk.1, bf16[2,3072,256]{2,1,0:T(8,128)(2,1)} %wv.1, ...), custom_call_target="tpu_custom_call" | custom-call | tf_op jit(solution)/shard_map/pallas_call | solution.py:393
  97.1 1.6 %reshape.20 = bf16[2,128,2,128]{3,2,1,0:T(2,128)(2,1)} reshape(bf16[2,128,256]{2,1,0:T(8,128)(2,1)} %get-tuple-element.7) | data formatting | bytes 262144 | tf_op jit(solution)/shard_map/reshape | solution.py:405
  98.6 1.6 %reshape.21 = bf16[2,128,2,128]{3,2,1,0:T(2,128)(2,1)} reshape(bf16[2,128,256]{2,1,0:T(8,128)(2,1)} %get-tuple-element.8) | data formatting | bytes 262144 | tf_op jit(solution)/shard_map/reshape | solution.py:405
  100.2 2.1 %copy.17 = bf16[128,3072]{1,0:T(8,128)(2,1)} copy(bf16[128,3072]{1,0:T(8,128)(2,1)} %get-tuple-element.12) | data formatting | bytes 1572864
